TPU v7x, 32 devices: a whole 2x2x4 slice. The times are simulated.
32 devices in a mesh: dp: 8 (over z, x), rep: 4 (over y, core).
Axes of the slice: x: 2, y: 2, z: 4, core: 2. Of those that a mesh axis runs over, the one named last changes fastest.
Arguments:
- token_inputs: bfloat16 [16384, 2048], P(('dp', 'rep')), may hold values from -12 to 12
- cotangent: bfloat16 [16384, 2048], P(('dp', 'rep')), may hold values from -6 to 6
- gate_preact: bfloat16 [16384, 768], P(('dp', 'rep')), may hold values from -6 to 6
- up_preact: bfloat16 [16384, 768], P(('dp', 'rep')), may hold values from -6 to 6
- down_weight: bfloat16 [2, 768, 2048], P(None, None, 'dp'), may hold values from -0.21875 to 0.21875
- block_expert: int32 [128], P(('dp', 'rep')), may hold values from 0 to 1
- block_count: int32 [128], P(('dp', 'rep')), may hold values from 1 to 128, as said below
Outputs:
- update: bfloat16 [2, 3, 768, 2048], P(None, None, None, 'dp')
Inputs may be any that keep to these rules, and one draw needn't show every extreme that they name: `block_count`: live rows of a block, at most 128; in every draw some block is full.
All inputs are finite; a program needn't handle non-finite values.
Results may differ from a plain program's by a relative error of at most 0.02.
Values may be sent and summed in bfloat16 or wider, within the bound.
A program may use at most 128 MiB of HBM per device.

v0:
```python
import math

import jax
import jax.numpy as jnp
from jax import lax
from jax.sharding import PartitionSpec as P

D = 2048
ITERS = 2


ns_first = 3.4445
ns_second = -4.775
ns_third = 2.0315
norm_eps = 1e-07


def whole_sweeps(matrix, column_width, groups_all, sweeps, scale):
    hidden_width = matrix.shape[0]
    group = math.gcd(8, groups_all)
    current = matrix
    result = None
    for sweep in range(sweeps):

        def add_group(index, total):
            cols = lax.dynamic_slice_in_dim(
                current, index * group * column_width, group * column_width, 1
            )
            cols = cols.reshape(hidden_width, group, column_width)
            term = jnp.einsum(
                "fnd,gnd->nfg", cols, cols, preferred_element_type=jnp.float32
            ).astype(jnp.bfloat16)
            return total + jnp.sum(lax.optimization_barrier(term).astype(jnp.float32), axis=0)

        gram = lax.fori_loop(
            0, groups_all // group, add_group, jnp.zeros((hidden_width, hidden_width), jnp.float32)
        )
        gram_half = gram.astype(jnp.bfloat16)
        squared = jnp.dot(gram_half, gram_half, preferred_element_type=jnp.float32)
        poly = (ns_second * gram + ns_third * squared).astype(jnp.bfloat16)
        newer = ns_first * current.astype(jnp.float32) + jnp.dot(
            poly, current, preferred_element_type=jnp.float32
        )
        if sweep + 1 < sweeps:
            current = newer.astype(jnp.bfloat16)
        else:
            result = (scale * newer).astype(jnp.bfloat16)
    return result


def per_device(
    token_inputs, cotangent, gate_preact, up_preact, down_weight, block_expert, block_count
):
    blocks = block_count.shape[0]
    rows_here = token_inputs.shape[0]
    hidden_width = gate_preact.shape[1]
    width = token_inputs.shape[1]
    block_rows = rows_here // blocks
    experts_here = down_weight.shape[0]
    row_place = jnp.arange(rows_here, dtype=jnp.int32) % block_rows
    row_count = jnp.repeat(block_count, block_rows, total_repeat_length=rows_here)
    row_expert = jnp.repeat(block_expert, block_rows, total_repeat_length=rows_here)
    live_rows = row_place < row_count
    masked = jnp.where(live_rows[:, None], cotangent, jnp.zeros_like(cotangent))
    gate = gate_preact.astype(jnp.float32)
    upper = up_preact.astype(jnp.float32)
    sigmoid_gate = jax.nn.sigmoid(gate)
    hidden = (gate * sigmoid_gate * upper).astype(jnp.bfloat16)
    selector = (row_expert[None, :] == jnp.arange(experts_here, dtype=jnp.int32)[:, None]).astype(
        jnp.bfloat16
    )
    masked_each = masked[None, :, :] * selector[:, :, None]
    weights_all = lax.all_gather(down_weight, "dp", axis=2, tiled=True)
    back = jnp.einsum("erd,efd->rf", masked_each, weights_all, preferred_element_type=jnp.float32)
    grad_gate = (back * upper * sigmoid_gate * (1.0 + gate * (1.0 - sigmoid_gate))).astype(
        jnp.bfloat16
    )
    grad_up = (back * gate * sigmoid_gate).astype(jnp.bfloat16)
    gate_up = jnp.concatenate([grad_gate, grad_up], axis=1)
    gate_up_each = gate_up[None, :, :] * selector[:, :, None]
    hidden_each = hidden[None, :, :] * selector[:, :, None]
    input_part = jnp.einsum(
        "erf,rd->efd", gate_up_each, token_inputs, preferred_element_type=jnp.float32
    )
    output_part = jnp.einsum("erf,rd->efd", hidden_each, masked, preferred_element_type=jnp.float32)
    partial_value = jnp.concatenate(
        [input_part.reshape(experts_here, 2, hidden_width, width), output_part[:, None]], axis=1
    )
    partial_half = partial_value.astype(jnp.bfloat16)
    terms = lax.optimization_barrier(partial_half).astype(jnp.float32)
    grad = lax.psum_scatter(
        terms.astype(jnp.bfloat16), "dp", scatter_dimension=3, tiled=True
    ).astype(jnp.float32)
    grad = lax.psum(grad.astype(jnp.bfloat16), "rep").astype(jnp.float32)
    squares = lax.psum(jnp.sum(grad * grad, axis=(2, 3)), "dp")
    current = (grad / (jnp.sqrt(squares) + norm_eps)[:, :, None, None]).astype(jnp.bfloat16)
    column_width = current.shape[3]
    scale = jnp.sqrt(jnp.float32(D))
    result = None
    n_dp = lax.axis_size("dp")
    matrices = experts_here * 3
    flat = current.reshape(matrices, hidden_width, column_width)
    padding = jnp.zeros((n_dp - matrices, hidden_width, column_width), jnp.bfloat16)
    outbound = jnp.concatenate([flat, padding], axis=0)
    owned = lax.all_to_all(outbound, "dp", split_axis=0, concat_axis=2, tiled=True)
    finished = whole_sweeps(owned[0], column_width, n_dp, ITERS, scale)
    returned = lax.all_to_all(finished[None], "dp", split_axis=2, concat_axis=0, tiled=True)
    result = returned[:matrices].reshape(experts_here, 3, hidden_width, column_width)
    return result


def solution(mesh):
    placed = (
        P(("dp", "rep"), None),
        P(("dp", "rep"), None),
        P(("dp", "rep"), None),
        P(("dp", "rep"), None),
        P(None, None, "dp"),
        P(("dp", "rep")),
        P(("dp", "rep")),
    )
    return jax.shard_map(
        per_device, mesh=mesh, in_specs=placed, out_specs=P(None, None, None, "dp"), check_vma=False
    )
```

profile of v0, /device:TPU:0, one launch (start us, length us, event | category | flops | bytes accessed | tf_op | source)
XLA Modules:
  0.0 795.3 jit_solution(15564926438498596758)
XLA Ops:
  6.5 0.0 copy-start
  6.5 0.0 all-gather.2.cloned.1.call-start
  6.5 0.7 all-gather.2.cloned.1.call-update
  7.3 0.0 reduce-scatter.2.cloned.1.call-start
  7.3 1.4 fusion.46
  8.7 2.5 fusion.34
  11.2 1.4 fusion.45
  12.6 2.5 select_select_fusion
  15.2 3.1 broadcast_select_fusion
  18.3 93.3 %all-gather.2.cloned.1.call-done = bf16[2,768,2048]{2,1,0:T(8,128)(2,1)} async-done(((bf16[2,768,256]{2,1,0:T(8,128)(2,1)}), bf16[2,768,2048]{2,1,0:T(8,128)(2,1)}) %all-gather.2.cloned.1.call-update) | async-done | bytes 6291472 | tf_op jit(solution)/shard_map/all_gather | solution.py:73
  111.6 7.8 fusion.15
  119.4 1.3 pad_maximum_fusion.1
  120.7 2.6 copy.31
  123.3 1.2 copy.32
  124.5 5.5 convert_bitcast_fusion
  129.9 0.0 copy-done
  130.0 0.0 copy-done.3
  130.0 6.9 convolution_convert_fusion
  136.9 10.4 %pad_maximum_fusion = bf16[2,3,768,2048]{3,2,1,0:T(8,128)(2,1)} fusion(bf16[2,1,768,2048]{3,2,1,0:T(8,128)(2,1)S(1)} %convert_bitcast_fusion, bf16[2,2,768,2048]{3,2,1,0:T(8,128)(2,1)S(1)} %bitcast.77), kind=kLoop, calls=%fused_computation | loop fusion | flops 9437184 | bytes 37748736 | tf_op jit(solution)/shard_map/concatenate | solution.py:86
  147.3 0.0 reduce-scatter.2.cloned.1.call-update
  147.4 0.0 all-reduce.3.cloned.1.call-start
  147.4 308.6 %reduce-scatter.2.cloned.1.call-done = bf16[2,3,768,256]{3,2,1,0:T(8,128)(2,1)} async-done(((bf16[2,3,768,2048]{3,2,1,0:T(8,128)(2,1)}), bf16[2,3,768,256]{3,2,1,0:T(8,128)(2,1)}) %reduce-scatter.2.cloned.1.call-update) | async-done | bytes 2359312 | tf_op jit(solution)/shard_map/reduce_scatter | solution.py:91
  456.1 0.0 all-reduce.3.cloned.1.call-update
  456.1 57.2 %all-reduce.3.cloned.1.call-done = bf16[2,3,768,256]{3,2,1,0:T(8,128)(2,1)} async-done(((bf16[2,3,768,256]{3,2,1,0:T(8,128)(2,1)}), bf16[2,3,768,256]{3,2,1,0:T(8,128)(2,1)}) %all-reduce.3.cloned.1.call-update) | async-done | bytes 2359312 | tf_op jit(solution)/shard_map/psum | solution.py:94
  513.2 2.5 fusion
  515.7 21.3 %psum.15 = f32[2,3]{1,0:T(2,128)S(1)} all-reduce(f32[2,3]{1,0:T(2,128)S(1)} %fusion), channel_id=1, replica_groups=mesh['dp'=8,'rep'=4] {'dp'}, use_global_device_ids=true, to_apply=%region_3.5 | all-reduce | flops 6 | bytes 48 | tf_op jit(solution)/shard_map/psum | solution.py:95
  537.0 0.0 copy-done.2
  537.0 0.9 fusion.1
  538.0 0.2 concatenate.18
  538.2 70.2 %all_to_all.30 = bf16[8,768,256]{2,1,0:T(8,128)(2,1)} all-to-all(bf16[8,768,256]{2,1,0:T(8,128)(2,1)S(1)} %concatenate.18), channel_id=1, replica_groups=mesh['dp'=8,'rep'=4] {'dp'}, dimensions={0} | all-to-all | bytes 6291456 | tf_op jit(solution)/shard_map/all_to_all | solution.py:105
  608.4 5.5 convolution_convert_fusion.2
  613.9 2.7 convert_reduce_fusion.1
  616.6 3.2 copy.34
  619.8 3.0 copy.35
  622.8 9.3 %add_convert_fusion = bf16[768,2048]{1,0:T(8,128)(2,1)} fusion(bf16[768,2048]{1,0:T(8,128)(2,1)} %copy.35, bf16[768,2048]{0,1:T(8,128)(2,1)S(1)} %bitcast.76, f32[768,768]{1,0:T(8,128)} %convert_reduce_fusion.1), kind=kOutput, calls=%fused_computation.7 | convolution fusion | flops 3331129344 | bytes 11796480 | tf_op jit(solution)/shard_map/dot_general | solution.py:41
  632.1 5.5 convolution_convert_fusion.1
  637.6 2.7 convert_reduce_fusion
  640.4 8.7 %fusion.8 = bf16[1,768,2048]{2,1,0:T(8,128)(2,1)S(1)} fusion(bf16[768,2048]{1,0:T(8,128)(2,1)} %add_convert_fusion, f32[768,768]{1,0:T(8,128)} %convert_reduce_fusion), kind=kOutput, calls=%fused_computation.19 | convolution fusion | flops 3332702208 | bytes 8650752 | tf_op jit(solution)/shard_map/dot_general | solution.py:41
  649.1 11.2 %copy.38 = bf16[1,768,2048]{1,0,2:T(2,128)(2,1)} copy(bf16[1,768,2048]{2,1,0:T(8,128)(2,1)S(1)} %fusion.8) | data formatting | bytes 6291456 | tf_op jit(solution)/shard_map/broadcast_in_dim | solution.py:107
  660.3 0.5 broadcast.198
  660.8 33.5 %reduce.3 = bf16[2048,768]{1,0:T(8,128)(2,1)} reduce(bf16[2048,1,768]{2,1,0:T(2,128)(2,1)} %bitcast.73, bf16[]{:T(256)} %broadcast.198), dimensions={1}, to_apply=%bitcast.67.reduce_sub_computation | reduce | bytes 6291458
  694.3 4.6 reshape.141
  699.0 72.8 %all_to_all.31 = bf16[8,2,98304]{2,1,0:T(2,128)(2,1)} all-to-all(bf16[8,2,98304]{2,1,0:T(2,128)(2,1)S(1)} %reshape.141), channel_id=1, replica_groups=mesh['dp'=8,'rep'=4] {'dp'}, dimensions={0} | all-to-all | bytes 6291456 | tf_op jit(solution)/shard_map/all_to_all | solution.py:107
  771.8 7.8 reshape.142
  779.6 3.3 copy.40
  782.9 0.0 copy-start.1
  782.9 1.6 slice.46
  784.5 4.3 copy.39
  (5 shorter events, 0.0 us)
Async XLA Ops:
  6.5 123.4 %copy-start = (bf16[512,2048]{1,0:T(8,128)(2,1)S(1)}, bf16[512,2048]{1,0:T(8,128)(2,1)}, u32[]{:S(2)}) copy-start(bf16[512,2048]{1,0:T(8,128)(2,1)} %param.13) | copy-start | bytes 6291460
  6.5 105.1 %all-gather.2.cloned.1.call-start = ((), (), s32[]{:S(2)}) async-start(), calls=%async_computation.3 | async-start | bytes 7077888 | tf_op jit(solution)/shard_map/all_gather | solution.py:73
  7.3 448.8 %reduce-scatter.2.cloned.1.call-start = ((), (), s32[]{:S(2)}) async-start(), calls=%async_computation.4 | async-start | bytes 21233664 | tf_op jit(solution)/shard_map/reduce_scatter | solution.py:91
  124.5 5.5 copy-start.3
  147.4 365.9 %all-reduce.3.cloned.1.call-start = ((), (), s32[]{:S(2)}) async-start(), calls=%async_computation.5 | async-start | bytes 4718592 | tf_op jit(solution)/shard_map/psum | solution.py:94
  513.2 23.8 %copy-start.2 = (bf16[2,3,768,256]{3,2,1,0:T(8,128)(2,1)S(1)}, bf16[2,3,768,256]{3,2,1,0:T(8,128)(2,1)}, u32[]{:S(2)}) copy-start(bf16[2,3,768,256]{3,2,1,0:T(8,128)(2,1)} %all-reduce.3.cloned.1.call-done) | copy-start | bytes 7077892
  782.9 5.9 copy-start.1
Sparse Core Ops, SparseCore 0:
  9.4 102.1 all-gather.1
  147.5 308.5 reduce-scatter.1
  458.4 54.7 all-reduce.2
where the time goes:
time: 796 us; the launch traced here: 795 us
  waiting for transfers between devices  460 us (58%)
  blocking collectives  164 us (21%)
  other arithmetic  62.2 us (8%)
  matrix products  49.2 us (6%)
  local copies, waits for them, and re-layouts  46.3 us (6%)
  between operations  13.2 us (2%)
    reduce_scatter x1, waiting for transfers between devices, per_device(): lax.psum_scatter(terms.astype(jnp.bfloat16), 'dp', scatter_dimension=3, t...  309 us
    all_gather x1, waiting for transfers between devices, per_device(): weights_all = lax.all_gather(down_weight, 'dp', axis=2, tiled=True)  93.3 us
    all_to_all x1, blocking collectives, per_device(): lax.all_to_all(finished[None], 'dp', split_axis=2, concat_axis=0, tiled=T...  72.8 us
    all_to_all x1, blocking collectives, per_device(): lax.all_to_all(outbound, 'dp', split_axis=0, concat_axis=2, tiled=True)  70.2 us
    psum x1, waiting for transfers between devices, per_device(): grad = lax.psum(grad.astype(jnp.bfloat16), 'rep').astype(jnp.float32)  57.2 us
    unnamed x1, other arithmetic  33.5 us
    psum x1, blocking collectives, per_device(): squares = lax.psum(jnp.sum(grad * grad, axis=(2, 3)), 'dp')  21.3 us
    dot_general x2, matrix products, whole_sweeps(): jnp.dot(poly, current, preferred_element_type=jnp.float32)  18 us
  transfers between devices with their start and end apart: 3, of which 3 were waited for; matrix products, arithmetic and copies ran while one was open for 1% of the time, Pallas kernels for 0%

commit v1 on v0

v1 whole, which is shorter than its diff:
```python
import functools

import jax
import jax.numpy as jnp
from jax import lax
from jax.experimental import pallas as pl
from jax.experimental.pallas import tpu as pltpu
from jax.sharding import PartitionSpec as P

D = 2048
ITERS = 2
MESH = pl.DeviceIdType.MESH

ns_first = 3.4445
ns_second = -4.775
ns_third = 2.0315
norm_eps = 1e-07


def rep_sum_kernel(
    n_chunks, parts, out, local, near, summed, far,
    load_sem, near_send, near_recv, far_send, far_recv, store_sem,
):
    dp = lax.axis_index("dp")
    rep = lax.axis_index("rep")
    pair = rep + 1 - 2 * lax.rem(rep, 2)
    other = lax.rem(rep + 2, 4)
    other_pair = lax.rem(pair + 2, 4)

    def near_copy(slot, chunk):
        part = other_pair if slot == 0 else pair
        return pltpu.make_async_remote_copy(
            src_ref=parts.at[part, chunk],
            dst_ref=near.at[slot, chunk],
            send_sem=near_send.at[slot, chunk],
            recv_sem=near_recv.at[slot, chunk],
            device_id=(dp, pair),
            device_id_type=MESH,
        )

    def load(slot, chunk):
        part = other if slot == 0 else rep
        return pltpu.make_async_copy(
            parts.at[part, chunk], local.at[slot, chunk], load_sem.at[slot, chunk]
        )

    def far_copy(chunk):
        return pltpu.make_async_remote_copy(
            src_ref=summed.at[chunk],
            dst_ref=far.at[chunk],
            send_sem=far_send.at[chunk],
            recv_sem=far_recv.at[chunk],
            device_id=(dp, other),
            device_id_type=MESH,
        )

    def store(chunk):
        return pltpu.make_async_copy(local.at[1, chunk], out.at[chunk], store_sem.at[chunk])

    for slot in range(2):

        @pl.loop(0, n_chunks)
        def _(chunk, slot=slot):
            near_copy(slot, chunk).start()
            load(slot, chunk).start()

    @pl.loop(0, n_chunks)
    def _(chunk):
        load(0, chunk).wait()
        near_copy(0, chunk).wait_recv()
        summed[chunk] = (
            local[0, chunk].astype(jnp.float32) + near[0, chunk].astype(jnp.float32)
        ).astype(jnp.bfloat16)
        far_copy(chunk).start()

    @pl.loop(0, n_chunks)
    def _(chunk):
        load(1, chunk).wait()
        near_copy(1, chunk).wait_recv()
        far_copy(chunk).wait_recv()
        local[1, chunk] = (
            local[1, chunk].astype(jnp.float32)
            + near[1, chunk].astype(jnp.float32)
            + far[chunk].astype(jnp.float32)
        ).astype(jnp.bfloat16)
        store(chunk).start()

    @pl.loop(0, n_chunks)
    def _(chunk):
        near_copy(0, chunk).wait_send()
        near_copy(1, chunk).wait_send()
        far_copy(chunk).wait_send()
        store(chunk).wait()


def rep_sum(value, rows):
    width = value.shape[-1]
    parts = value.reshape(4, -1, rows, width)
    n_chunks = parts.shape[1]
    block = (n_chunks, rows, width)
    summed = pl.pallas_call(
        functools.partial(rep_sum_kernel, n_chunks),
        out_shape=jax.ShapeDtypeStruct(block, jnp.bfloat16),
        in_specs=[pl.BlockSpec(memory_space=pl.ANY)],
        out_specs=pl.BlockSpec(memory_space=pl.ANY),
        scratch_shapes=[
            pltpu.VMEM((2,) + block, jnp.bfloat16),
            pltpu.VMEM((2,) + block, jnp.bfloat16),
            pltpu.VMEM(block, jnp.bfloat16),
            pltpu.VMEM(block, jnp.bfloat16),
            pltpu.SemaphoreType.DMA((2, n_chunks)),
            pltpu.SemaphoreType.DMA((2, n_chunks)),
            pltpu.SemaphoreType.DMA((2, n_chunks)),
            pltpu.SemaphoreType.DMA((n_chunks,)),
            pltpu.SemaphoreType.DMA((n_chunks,)),
            pltpu.SemaphoreType.DMA((n_chunks,)),
        ],
        compiler_params=pltpu.CompilerParams(has_side_effects=True),
        cost_estimate=pl.CostEstimate(
            flops=value.size * 1000, bytes_accessed=value.size * 2, transcendentals=0
        ),
    )(parts)
    return summed.reshape(n_chunks * rows, width)


def column_block(matrix, source, width, rows=None):
    if len(matrix.shape) == 3:
        return matrix.at[source] if rows is None else matrix.at[source, rows]
    start = source * width
    cols = pl.ds(start if isinstance(start, int) else pl.multiple_of(start, width), width)
    return matrix.at[:, cols] if rows is None else matrix.at[rows, cols]


def gather_kernel(n_dp, first, second, whole, full_send, half_send, full_recv, half_recv):
    dp = lax.axis_index("dp")
    rep = lax.axis_index("rep")
    odd = lax.rem(rep, 2)
    hidden, width = first.shape
    half = second.shape[0]
    owner = n_dp // 4

    def full_copy(source):
        return pltpu.make_async_remote_copy(
            src_ref=first,
            dst_ref=column_block(whole, source, width),
            send_sem=full_send,
            recv_sem=full_recv.at[source],
            device_id=(owner + odd, rep),
            device_id_type=MESH,
        )

    def half_copy(place, source):
        rows = pl.ds(pl.multiple_of(place * half, half), half)
        return pltpu.make_async_remote_copy(
            src_ref=second,
            dst_ref=column_block(whole, source, width, rows),
            send_sem=half_send,
            recv_sem=half_recv.at[place, source],
            device_id=(owner + 2, rep - odd),
            device_id_type=MESH,
        )

    own_full = pltpu.make_async_copy(first, column_block(whole, dp, width), full_send)
    own_half = pltpu.make_async_copy(
        second, column_block(whole, dp, width, pl.ds(0, half)), half_send
    )
    is_full = dp == owner + odd
    is_half = jnp.logical_and(dp == owner + 2, odd == 0)

    @pl.when(is_full)
    def _():
        own_full.start()

    @pl.when(jnp.logical_not(is_full))
    def _():
        full_copy(dp).start()

    @pl.when(is_half)
    def _():
        own_half.start()

    @pl.when(jnp.logical_not(is_half))
    def _():
        half_copy(odd, dp).start()

    @pl.when(is_full)
    def _():
        own_full.wait()
        for source in range(n_dp):

            @pl.when(dp != source)
            def _(source=source):
                full_copy(source).wait_recv()

    @pl.when(jnp.logical_not(is_full))
    def _():
        full_copy(dp).wait_send()

    @pl.when(is_half)
    def _():
        own_half.wait()
        for source in range(n_dp):
            half_copy(1, source).wait_recv()

            @pl.when(dp != source)
            def _(source=source):
                half_copy(0, source).wait_recv()

    @pl.when(jnp.logical_not(is_half))
    def _():
        half_copy(odd, dp).wait_send()


def gather_matrix(first, second, n_dp):
    hidden, width = first.shape
    blocked = width % 128 != 0
    shape = (n_dp, hidden, width) if blocked else (hidden, width * n_dp)
    whole = pl.pallas_call(
        functools.partial(gather_kernel, n_dp),
        out_shape=jax.ShapeDtypeStruct(shape, jnp.bfloat16),
        in_specs=[pl.BlockSpec(memory_space=pltpu.VMEM)] * 2,
        out_specs=pl.BlockSpec(memory_space=pltpu.VMEM),
        scratch_shapes=[
            pltpu.SemaphoreType.DMA,
            pltpu.SemaphoreType.DMA,
            pltpu.SemaphoreType.DMA((n_dp,)),
            pltpu.SemaphoreType.DMA((2, n_dp)),
        ],
        compiler_params=pltpu.CompilerParams(has_side_effects=True),
    )(first, second)
    return whole.transpose(1, 0, 2).reshape(hidden, width * n_dp) if blocked else whole


def spread_kernel(n_dp, matrix, out, held, owner_send, pair_send, far_send, recv, store_sem):
    dp = lax.axis_index("dp")
    rep = lax.axis_index("rep")
    hidden, width = held.shape[1:]
    owner = n_dp // 4
    pair = rep + 1 - 2 * lax.rem(rep, 2)
    other = lax.rem(rep + 2, 4)
    kinds = 3
    matrices = [(expert, kind) for expert in range(2) for kind in range(kinds)]

    def remote(source, index, send_sem, device):
        return pltpu.make_async_remote_copy(
            src_ref=source,
            dst_ref=held.at[index],
            send_sem=send_sem,
            recv_sem=recv.at[index],
            device_id=device,
            device_id_type=MESH,
        )

    def store(index):
        return pltpu.make_async_copy(held.at[index], out.at[index], store_sem.at[index])

    def root_of(expert, kind):
        return 2 * expert + kind % 2

    for index, (expert, kind) in enumerate(matrices):

        @pl.when(jnp.logical_and(dp == owner + kind, rep == root_of(expert, kind)))
        def _(index=index, kind=kind):
            for target in range(n_dp):
                block = column_block(matrix, target, width)

                @pl.when(dp != target)
                def _(target=target, block=block):
                    remote(block, index, owner_send.at[target], (target, rep)).start()

                @pl.when(dp == target)
                def _(target=target, block=block):
                    pltpu.make_async_copy(
                        block, held.at[index], owner_send.at[target]
                    ).start()

    def arrived(index, expert, kind):
        here = dp == owner + kind

        @pl.when(here)
        def _():
            pltpu.make_async_copy(
                column_block(matrix, dp, width),
                held.at[index],
                owner_send.at[dp],
            ).wait()

        @pl.when(jnp.logical_not(here))
        def _():
            remote(held.at[index], index, pair_send.at[index], (dp, pair)).wait_recv()

    for index, (expert, kind) in enumerate(matrices):

        @pl.when(rep == root_of(expert, kind))
        def _(index=index, expert=expert, kind=kind):
            arrived(index, expert, kind)
            remote(held.at[index], index, far_send.at[index], (dp, other)).start()
            remote(held.at[index], index, pair_send.at[index], (dp, pair)).start()
            store(index).start()

    for index, (expert, kind) in enumerate(matrices):

        @pl.when(other == root_of(expert, kind))
        def _(index=index):
            remote(held.at[index], index, pair_send.at[index], (dp, pair)).wait_recv()
            remote(held.at[index], index, pair_send.at[index], (dp, pair)).start()
            store(index).start()

    for index, (expert, kind) in enumerate(matrices):
        root = root_of(expert, kind)

        @pl.when(jnp.logical_and(rep != root, other != root))
        def _(index=index):
            remote(held.at[index], index, pair_send.at[index], (dp, pair)).wait_recv()
            store(index).start()

    for index, (expert, kind) in enumerate(matrices):
        root = root_of(expert, kind)

        @pl.when(jnp.logical_and(dp == owner + kind, rep == root))
        def _(index=index):
            for target in range(n_dp):

                @pl.when(dp != target)
                def _(target=target):
                    remote(
                        column_block(matrix, target, width),
                        index,
                        owner_send.at[target],
                        (target, rep),
                    ).wait_send()

        @pl.when(rep == root)
        def _(index=index):
            remote(held.at[index], index, far_send.at[index], (dp, other)).wait_send()

        @pl.when(jnp.logical_or(rep == root, other == root))
        def _(index=index):
            remote(held.at[index], index, pair_send.at[index], (dp, pair)).wait_send()

        store(index).wait()


def spread_matrix(matrix, n_dp):
    hidden, width = matrix.shape[0], matrix.shape[1] // n_dp
    if width % 128 != 0:
        matrix = matrix.reshape(hidden, n_dp, width).transpose(1, 0, 2)
    return pl.pallas_call(
        functools.partial(spread_kernel, n_dp),
        out_shape=jax.ShapeDtypeStruct((6, hidden, width), jnp.bfloat16),
        in_specs=[pl.BlockSpec(memory_space=pltpu.VMEM)],
        out_specs=pl.BlockSpec(memory_space=pl.ANY),
        scratch_shapes=[
            pltpu.VMEM((6, hidden, width), jnp.bfloat16),
            pltpu.SemaphoreType.DMA((n_dp,)),
            pltpu.SemaphoreType.DMA((6,)),
            pltpu.SemaphoreType.DMA((6,)),
            pltpu.SemaphoreType.DMA((6,)),
            pltpu.SemaphoreType.DMA((6,)),
        ],
        compiler_params=pltpu.CompilerParams(has_side_effects=True),
    )(matrix)


def whole_sweeps(grad, sweeps, scale):
    as_float = grad.astype(jnp.float32)
    norm = jnp.sqrt(jnp.sum(as_float * as_float)) + norm_eps
    current = (as_float / norm).astype(jnp.bfloat16)
    result = None
    for sweep in range(sweeps):
        gram = jnp.einsum("fd,gd->fg", current, current, preferred_element_type=jnp.float32)
        gram_half = gram.astype(jnp.bfloat16)
        squared = jnp.dot(gram_half, gram_half, preferred_element_type=jnp.float32)
        poly = (ns_second * gram + ns_third * squared).astype(jnp.bfloat16)
        newer = ns_first * current.astype(jnp.float32) + jnp.dot(
            poly, current, preferred_element_type=jnp.float32
        )
        if sweep + 1 < sweeps:
            current = newer.astype(jnp.bfloat16)
        else:
            result = (scale * newer).astype(jnp.bfloat16)
    return result


def per_device(
    token_inputs, cotangent, gate_preact, up_preact, down_weight, block_expert, block_count
):
    n_dp = lax.axis_size("dp")
    rep = lax.axis_index("rep")
    odd = lax.rem(rep, 2)
    blocks = block_count.shape[0]
    rows_here = token_inputs.shape[0]
    hidden_width = gate_preact.shape[1]
    half = hidden_width // 2
    width = token_inputs.shape[1]
    block_rows = rows_here // blocks
    experts_here = down_weight.shape[0]

    own_half = lax.dynamic_slice_in_dim(down_weight, odd * half, half, 1)
    weights_own = lax.all_gather(own_half, "dp", axis=2, tiled=True)

    row_place = jnp.arange(rows_here, dtype=jnp.int32) % block_rows
    row_count = jnp.repeat(block_count, block_rows, total_repeat_length=rows_here)
    row_expert = jnp.repeat(block_expert, block_rows, total_repeat_length=rows_here)
    live_rows = row_place < row_count
    masked = jnp.where(live_rows[:, None], cotangent, jnp.zeros_like(cotangent))
    gate = gate_preact.astype(jnp.float32)
    upper = up_preact.astype(jnp.float32)
    sigmoid_gate = jax.nn.sigmoid(gate)
    hidden = (gate * sigmoid_gate * upper).astype(jnp.bfloat16)
    selector = (row_expert[None, :] == jnp.arange(experts_here, dtype=jnp.int32)[:, None]).astype(
        jnp.bfloat16
    )
    hidden_each = hidden[None, :, :] * selector[:, :, None]
    output_part = jnp.einsum(
        "erf,rd->efd", hidden_each, masked, preferred_element_type=jnp.float32
    ).astype(jnp.bfloat16)
    output_sum = rep_sum(output_part, 128)
    weights_own, output_sum = lax.optimization_barrier((weights_own, output_sum))
    pairs = [(0, 1), (1, 0), (2, 3), (3, 2)]
    weights_pair = lax.ppermute(weights_own, "rep", pairs)
    output_grad = lax.psum_scatter(output_sum, "dp", scatter_dimension=1, tiled=True)

    masked_each = masked[None, :, :] * selector[:, :, None]
    lower = jnp.where(odd == 0, weights_own, weights_pair)
    higher = jnp.where(odd == 0, weights_pair, weights_own)
    weights_all = jnp.concatenate([lower, higher], axis=1)
    back = jnp.einsum("erd,efd->rf", masked_each, weights_all, preferred_element_type=jnp.float32)
    grad_gate = (back * upper * sigmoid_gate * (1.0 + gate * (1.0 - sigmoid_gate))).astype(
        jnp.bfloat16
    )
    grad_up = (back * gate * sigmoid_gate).astype(jnp.bfloat16)
    gate_up = jnp.concatenate([grad_gate, grad_up], axis=1)
    gate_up_each = gate_up[None, :, :] * selector[:, :, None]
    input_part = jnp.einsum(
        "erf,rd->efd", gate_up_each, token_inputs, preferred_element_type=jnp.float32
    ).astype(jnp.bfloat16)
    input_sum = rep_sum(input_part, 128)
    input_grad = lax.psum_scatter(input_sum, "dp", scatter_dimension=1, tiled=True)

    whole = gather_matrix(input_grad, output_grad, n_dp)
    finished = whole_sweeps(whole, ITERS, jnp.sqrt(jnp.float32(D)))
    spread = spread_matrix(finished, n_dp)
    return spread.reshape(experts_here, 3, hidden_width, width // n_dp)


def solution(mesh):
    placed = (
        P(("dp", "rep"), None),
        P(("dp", "rep"), None),
        P(("dp", "rep"), None),
        P(("dp", "rep"), None),
        P(None, None, "dp"),
        P(("dp", "rep")),
        P(("dp", "rep")),
    )
    return jax.shard_map(
        per_device, mesh=mesh, in_specs=placed, out_specs=P(None, None, None, "dp"), check_vma=False
    )
```

time: 796 us -> 371 us (0.47)
  waiting for transfers between devices: 460 us -> 83.9 us
  Pallas kernels: 0 us -> 184 us
  blocking collectives: 164 us -> 0 us
  other arithmetic: 62.2 us -> 17.2 us
  local copies, waits for them, and re-layouts: 46.3 us -> 10.4 us
    reduce_scatter x1 -> x2, waiting for transfers between devices: 309 us -> 75.3 us  [the longest x1 75.2 us: per_device(): lax.psum_scatter(input_sum, 'dp', scatter_dimension=1, tiled=True)]
    pallas_call x0 -> x4, Pallas kernels: none -> 184 us  [the longest x2 123 us: rep_sum(): pl.pallas_call(functools.partial(rep_sum_kernel, n_chunks), out_shape=jax...]
    all_to_all x2 -> x0, blocking collectives: 143 us -> none  [the longest x1 72.8 us: per_device(): lax.all_to_all(finished[None], 'dp', split_axis=2, concat_axis=0, tiled=T...]
    all_gather x1, waiting for transfers between devices: 93.3 us -> 2.73 us  [per_device(): weights_own = lax.all_gather(own_half, 'dp', axis=2, tiled=True)]
    psum x1 -> x0, waiting for transfers between devices: 57.2 us -> none  [per_device(): grad = lax.psum(grad.astype(jnp.bfloat16), 'rep').astype(jnp.float32)]
    unnamed x1 -> x0, other arithmetic: 33.5 us -> none
    psum x1 -> x0, blocking collectives: 21.3 us -> none  [per_device(): squares = lax.psum(jnp.sum(grad * grad, axis=(2, 3)), 'dp')]
    unnamed x12 -> x19, local copies, waits for them, and re-layouts: 16.2 us -> 3.42 us
  transfers between devices with their start and end apart: 3 -> 4, of which waited for: 3 -> 3; matrix products, arithmetic and copies ran while one was open for 1% -> 10% of each run, Pallas kernels for 0% -> 34%
where the time goes in v1:
time: 371 us; the launch traced here: 365 us
  Pallas kernels  184 us (50%)
  waiting for transfers between devices  83.9 us (23%)
  matrix products  55.4 us (15%)
  other arithmetic  17.2 us (5%)
  between operations  14 us (4%)
  local copies, waits for them, and re-layouts  10.4 us (3%)
    pallas_call x2, Pallas kernels, rep_sum(): pl.pallas_call(functools.partial(rep_sum_kernel, n_chunks), out_shape=jax...  123 us
    reduce_scatter x1, waiting for transfers between devices, per_device(): lax.psum_scatter(input_sum, 'dp', scatter_dimension=1, tiled=True)  75.2 us
    pallas_call x1, Pallas kernels, spread_matrix(): pl.pallas_call(functools.partial(spread_kernel, n_dp), out_shape=jax.Shap...  40.8 us
    dot_general x2, matrix products, whole_sweeps(): jnp.dot(poly, current, preferred_element_type=jnp.float32)  21.6 us
    pallas_call x1, Pallas kernels, gather_matrix(): pl.pallas_call(functools.partial(gather_kernel, n_dp), out_shape=jax.Shap...  19.8 us
    dot_general x2, matrix products, whole_sweeps(): jnp.einsum('fd,gd->fg', current, current, preferred_element_type=jnp.floa...  13.8 us
    dot_general x1, matrix products, per_device(): jnp.einsum('erf,rd->efd', gate_up_each, token_inputs, preferred_element_t...  10.7 us
  transfers between devices with their start and end apart: 4, of which 3 were waited for; matrix products, arithmetic and copies ran while one was open for 10% of the time, Pallas kernels for 34%

profile of v1, /device:TPU:0, one launch (start us, length us, event | category | flops | bytes accessed | tf_op | source)
XLA Modules:
  0.0 365.0 jit_solution(9455237055221638925)
XLA Ops:
  6.5 0.0 copy-start
  6.5 0.0 all-gather.2.cloned.1.call-start
  6.5 1.9 constant_dynamic-slice_fusion
  8.5 0.0 all-gather.2.cloned.1.call-update
  8.5 0.0 reduce-scatter.5.cloned.1.call-start
  8.5 1.9 fusion.12
  10.4 1.2 copy.8
  11.6 0.0 copy-done.7
  11.6 0.6 fusion.48
  12.2 2.4 fusion.33
  14.7 0.0 copy-done.8
  14.7 0.6 fusion.49
  15.3 2.4 select_select_fusion
  17.8 1.9 broadcast_select_fusion.2
  19.6 0.0 copy-done.4
  19.6 0.0 copy-start.2
  19.7 5.3 %convolution_convert_fusion.1 = bf16[2,768,2048]{2,1,0:T(8,128)(2,1)} fusion(bf16[512,2048]{1,0:T(8,128)(2,1)S(1)} %broadcast_select_fusion.2, bf16[2,512]{1,0:T(2,128)(2,1)S(1)} %compare_convert_fusion, bf16[512,768]{0,1:T(8,128)(2,1)S(1)} %copy-done.4), kind=kOutput, calls=%fused_computation.11 | convolution fusion | flops 3225157632 | bytes 9177088 | tf_op jit(solution)/shard_map/erf,rd->efd/dot_general | solution.py:415
  25.0 0.0 copy-done.2
  25.0 47.1 %shard_map.73 = bf16[3,128,2048]{2,1,0:T(8,128)(2,1)} custom-call(bf16[4,3,128,2048]{3,2,1,0:T(8,128)(2,1)} %bitcast.55), custom_call_target="tpu_custom_call" | custom-call | flops 3145728000 | bytes 6291456 | tf_op jit(solution)/shard_map/pallas_call | solution.py:101
  72.1 2.7 all-gather.2.cloned.1.call-done
  74.8 0.0 collective-permute-start
  74.8 0.0 reduce-scatter.5.cloned.1.call-update
  74.8 0.0 copy-start.5
  74.8 0.0 reduce-scatter.3.cloned.1.call-start
  74.9 0.0 copy-start.3
  74.9 0.0 copy-start.6
  74.9 5.9 %collective-permute-done = bf16[2,384,2048]{2,1,0:T(8,128)(2,1)} collective-permute-done((bf16[2,384,2048]{2,1,0:T(8,128)(2,1)}, bf16[2,384,2048]{2,1,0:T(8,128)(2,1)}, u32[]{:S(2)}, u32[]{:S(2)}) %collective-permute-start) | collective-permute-done | bytes 3145760 | tf_op jit(solution)/shard_map/ppermute | solution.py:421
  80.8 3.3 broadcast_select_fusion.1
  84.1 0.0 copy-done.5
  84.1 0.0 copy-done.3
  84.1 0.0 copy-done.6
  84.1 4.0 %fusion.15 = (bf16[512,768]{1,0:T(8,128)(2,1)S(1)}, bf16[512,768]{1,0:T(8,128)(2,1)S(1)}) fusion(bf16[512,768]{1,0:T(8,128)(2,1)S(1)} %copy-done.5, bf16[512,768]{1,0:T(8,128)(2,1)S(1)} %copy-done.6, bf16[2,384,2048]{2,1,0:T(8,128)(2,1)S(1)} %get-tuple-element.31, bf16[2,384,2048]{2,1,0:T(8,128)(2,1)S(1)} %get-tuple-element.30, ...), kind=kOutput, calls=%fused_computation.32 | convolution fusion | flops 3241803776 | bytes 11536384 | tf_op jit(solution)/shard_map/erd,efd->rf/dot_general | solution.py:428
  88.1 1.3 pad_maximum_fusion
  89.4 2.6 copy.9
  92.0 10.7 %convolution_convert_fusion = bf16[2,1536,2048]{2,1,0:T(8,128)(2,1)} fusion(bf16[512,2048]{1,0:T(8,128)(2,1)S(1)} %copy-done, bf16[2,512]{1,0:T(2,128)(2,1)S(1)} %compare_convert_fusion, bf16[512,1536]{0,1:T(8,128)(2,1)} %copy.9), kind=kOutput, calls=%fused_computation | convolution fusion | flops 6450315264 | bytes 16254976 | tf_op jit(solution)/shard_map/erf,rd->efd/dot_general | solution.py:435
  102.6 76.4 %shard_map.74 = bf16[6,128,2048]{2,1,0:T(8,128)(2,1)} custom-call(bf16[4,6,128,2048]{3,2,1,0:T(8,128)(2,1)} %bitcast.54), custom_call_target="tpu_custom_call" | custom-call | flops 6291456000 | bytes 12582912 | tf_op jit(solution)/shard_map/pallas_call | solution.py:101
  179.1 0.0 reduce-scatter.3.cloned.1.call-update
  179.1 0.0 reduce-scatter.5.cloned.1.call-done.second
  179.1 75.2 %reduce-scatter.3.cloned.1.call-done.first = bf16[768,256]{1,0:T(8,128)(2,1)} async-done(((bf16[768,2048]{1,0:T(8,128)(2,1)}), bf16[768,256]{1,0:T(8,128)(2,1)}) %reduce-scatter.3.cloned.1.call-update) | async-done | bytes 393232 | tf_op jit(solution)/shard_map/reduce_scatter | solution.py:439
  254.3 19.8 %shard_map.75 = bf16[768,2048]{1,0:T(8,128)(2,1)} custom-call(bf16[768,256]{1,0:T(8,128)(2,1)} %reduce-scatter.3.cloned.1.call-done.first, bf16[384,256]{1,0:T(8,128)(2,1)} %reduce-scatter.5.cloned.1.call-done.second), custom_call_target="tpu_custom_call" | custom-call | tf_op jit(solution)/shard_map/pallas_call | solution.py:218
  274.1 4.1 %fusion = f32[]{:T(128)} fusion(bf16[768,2048]{1,0:T(8,128)(2,1)} %shard_map.75), kind=kLoop, calls=%fused_computation.3 | loop fusion | flops 4718591 | bytes 3145732 | tf_op jit(solution)/shard_map/reduce_sum | solution.py:367
  278.9 6.9 %fusion.45 = f32[768,768]{1,0:T(8,128)} fusion(bf16[768,2048]{1,0:T(8,128)(2,1)} %shard_map.75, f32[]{:T(128)S(6)} %add.54), kind=kOutput, calls=%fused_computation.66 | convolution fusion | flops 2420637696 | bytes 5505028 | tf_op jit(solution)/shard_map/fd,gd->fg/dot_general | solution.py:371
  285.9 11.3 %add_convert_fusion = bf16[768,2048]{1,0:T(8,128)(2,1)} fusion(f32[768,768]{1,0:T(8,128)} %fusion.45, f32[]{:T(128)S(6)} %add.54, bf16[768,2048]{1,0:T(8,128)(2,1)} %shard_map.75), kind=kOutput, calls=%fused_computation.10 | convolution fusion | flops 3340566528 | bytes 8650756 | tf_op jit(solution)/shard_map/dot_general | solution.py:375
  297.2 6.9 %fusion.50 = f32[768,768]{1,0:T(8,128)} fusion(bf16[768,2048]{1,0:T(8,128)(2,1)} %add_convert_fusion), kind=kOutput, calls=%fused_computation.69 | convolution fusion | flops 2415919104 | bytes 5505024 | tf_op jit(solution)/shard_map/fd,gd->fg/dot_general | solution.py:371
  304.1 10.2 %multiply_convert_fusion.matrix = bf16[768,2048]{1,0:T(8,128)(2,1)} fusion(bf16[768,2048]{1,0:T(8,128)(2,1)} %add_convert_fusion, f32[768,768]{1,0:T(8,128)} %fusion.50), kind=kOutput, calls=%fused_computation.9 | convolution fusion | flops 3332702208 | bytes 8650752 | tf_op jit(solution)/shard_map/dot_general | solution.py:375
  314.3 40.8 %shard_map.76 = bf16[6,768,256]{2,1,0:T(8,128)(2,1)} custom-call(bf16[768,2048]{1,0:T(8,128)(2,1)} %multiply_convert_fusion.matrix), custom_call_target="tpu_custom_call" | custom-call | tf_op jit(solution)/shard_map/pallas_call | solution.py:348
  355.1 0.0 copy-start.1
  355.1 3.4 copy.11
  (6 shorter events, 0.0 us)
Async XLA Ops:
  6.5 85.4 %copy-start = (bf16[512,2048]{1,0:T(8,128)(2,1)S(1)}, bf16[512,2048]{1,0:T(8,128)(2,1)}, u32[]{:S(2)}) copy-start(bf16[512,2048]{1,0:T(8,128)(2,1)} %param.13) | copy-start | bytes 6291460
  6.5 68.2 %all-gather.2.cloned.1.call-start = ((), (), s32[]{:S(2)}) async-start(), calls=%async_computation.2 | async-start | bytes 3538944 | tf_op jit(solution)/shard_map/all_gather | solution.py:400
  8.5 3.1 copy-start.7
  8.5 6.2 %copy-start.8 = (s32[4]{0:T(128)S(1)}, s32[4]{0:T(128)}, u32[]{:S(2)}) copy-start(s32[4]{0:T(128)} %param.18) | copy-start | bytes 52
  8.5 170.6 %reduce-scatter.5.cloned.1.call-start = ((), (), s32[]{:S(2)}) async-start(), calls=%async_computation.4 | async-start | bytes 1769472 | tf_op jit(solution)/shard_map/reduce_scatter | solution.py:422
  11.6 8.1 %copy-start.4 = (bf16[512,768]{0,1:T(8,128)(2,1)S(1)}, bf16[512,768]{0,1:T(8,128)(2,1)}, u32[]{:S(2)}) copy-start(bf16[512,768]{0,1:T(8,128)(2,1)} %copy.8) | copy-start | bytes 2359300
  19.6 5.3 %copy-start.2 = (bf16[512,2048]{1,0:T(8,128)(2,1)}, bf16[512,2048]{1,0:T(8,128)(2,1)S(1)}, u32[]{:S(2)}) copy-start(bf16[512,2048]{1,0:T(8,128)(2,1)S(1)} %broadcast_select_fusion.2) | copy-start | bytes 6291460
  74.8 6.0 %collective-permute-start = (bf16[2,384,2048]{2,1,0:T(8,128)(2,1)}, bf16[2,384,2048]{2,1,0:T(8,128)(2,1)}, u32[]{:S(2)}, u32[]{:S(2)}) collective-permute-start(bf16[2,384,2048]{2,1,0:T(8,128)(2,1)} %all-gather.2.cloned.1.call-done), channel_id=1, source_target_pairs={{0,1},{1,0},{2,3},{3,2},{4,5},{5,4},{6,7},{7,6},{8,9},{9,8},{10,11... | collective-permute-start | bytes 9437192 | tf_op jit(solution)/shard_map/ppermute | solution.py:421
  74.8 9.2 %copy-start.5 = (bf16[512,768]{1,0:T(8,128)(2,1)S(1)}, bf16[512,768]{1,0:T(8,128)(2,1)}, u32[]{:S(2)}) copy-start(bf16[512,768]{1,0:T(8,128)(2,1)} %param.16) | copy-start | bytes 2359300
  74.8 179.5 %reduce-scatter.3.cloned.1.call-start = ((), (), s32[]{:S(2)}) async-start(), calls=%async_computation.3 | async-start | bytes 3538944 | tf_op jit(solution)/shard_map/reduce_scatter | solution.py:439
  74.9 9.2 %copy-start.3 = (bf16[512,2048]{1,0:T(8,128)(2,1)S(1)}, bf16[512,2048]{1,0:T(8,128)(2,1)}, u32[]{:S(2)}) copy-start(bf16[512,2048]{1,0:T(8,128)(2,1)} %copy-done.2) | copy-start | bytes 6291460
  74.9 9.2 %copy-start.6 = (bf16[512,768]{1,0:T(8,128)(2,1)S(1)}, bf16[512,768]{1,0:T(8,128)(2,1)}, u32[]{:S(2)}) copy-start(bf16[512,768]{1,0:T(8,128)(2,1)} %param.15) | copy-start | bytes 2359300
  355.1 3.4 copy-start.1
Sparse Core Ops, SparseCore 0:
  9.4 65.3 all-gather.1
  78.2 64.6 reduce-scatter.4
  179.2 75.0 reduce-scatter.2

commit v2 on v1

--- a/solution.py
+++ b/solution.py
@@ -123,6 +123,146 @@
     return summed.reshape(n_chunks * rows, width)
 
 
+def full_sum_kernel(
+    n_chunks, n_dp, parts, out, local, near, summed, far, blocks,
+    load_sem, near_send, near_recv, far_send, far_recv, block_send, block_recv,
+):
+    dp = lax.axis_index("dp")
+    rep = lax.axis_index("rep")
+    pair = rep + 1 - 2 * lax.rem(rep, 2)
+    other = lax.rem(rep + 2, 4)
+    other_pair = lax.rem(pair + 2, 4)
+    width = blocks.shape[-1]
+
+    def near_copy(slot, chunk):
+        part = other_pair if slot == 0 else pair
+        return pltpu.make_async_remote_copy(
+            src_ref=parts.at[part, chunk],
+            dst_ref=near.at[slot, chunk],
+            send_sem=near_send.at[slot, chunk],
+            recv_sem=near_recv.at[slot, chunk],
+            device_id=(dp, pair),
+            device_id_type=MESH,
+        )
+
+    def load(slot, chunk):
+        part = other if slot == 0 else rep
+        return pltpu.make_async_copy(
+            parts.at[part, chunk], local.at[slot, chunk], load_sem.at[slot, chunk]
+        )
+
+    def far_copy(chunk):
+        return pltpu.make_async_remote_copy(
+            src_ref=summed.at[chunk],
+            dst_ref=far.at[chunk],
+            send_sem=far_send.at[chunk],
+            recv_sem=far_recv.at[chunk],
+            device_id=(dp, other),
+            device_id_type=MESH,
+        )
+
+    def columns(block):
+        return pl.ds(pl.multiple_of(block * width, width), width)
+
+    def block_copy(chunk, target, source):
+        return pltpu.make_async_remote_copy(
+            src_ref=local.at[1, chunk, :, columns(target)],
+            dst_ref=blocks.at[chunk, source],
+            send_sem=block_send.at[chunk, target],
+            recv_sem=block_recv.at[chunk, source],
+            device_id=(target, rep),
+            device_id_type=MESH,
+        )
+
+    def own_copy(chunk):
+        return pltpu.make_async_copy(
+            local.at[1, chunk, :, columns(dp)], blocks.at[chunk, dp], block_recv.at[chunk, dp]
+        )
+
+    for slot in range(2):
+
+        @pl.loop(0, n_chunks)
+        def _(chunk, slot=slot):
+            near_copy(slot, chunk).start()
+            load(slot, chunk).start()
+
+    @pl.loop(0, n_chunks)
+    def _(chunk):
+        load(0, chunk).wait()
+        near_copy(0, chunk).wait_recv()
+        summed[chunk] = (
+            local[0, chunk].astype(jnp.float32) + near[0, chunk].astype(jnp.float32)
+        ).astype(jnp.bfloat16)
+        far_copy(chunk).start()
+
+    @pl.loop(0, n_chunks)
+    def _(chunk):
+        load(1, chunk).wait()
+        near_copy(1, chunk).wait_recv()
+        far_copy(chunk).wait_recv()
+        local[1, chunk] = (
+            local[1, chunk].astype(jnp.float32)
+            + near[1, chunk].astype(jnp.float32)
+            + far[chunk].astype(jnp.float32)
+        ).astype(jnp.bfloat16)
+        for step in range(1, n_dp):
+            block_copy(chunk, lax.rem(dp + step, n_dp), dp).start()
+        own_copy(chunk).start()
+
+    @pl.loop(0, n_chunks)
+    def _(chunk):
+        own_copy(chunk).wait()
+        for step in range(1, n_dp):
+            block_copy(chunk, dp, lax.rem(dp + step, n_dp)).wait_recv()
+        total = blocks[chunk, 0].astype(jnp.float32)
+        for source in range(1, n_dp):
+            total = total + blocks[chunk, source].astype(jnp.float32)
+        out[chunk] = total.astype(jnp.bfloat16)
+
+    @pl.loop(0, n_chunks)
+    def _(chunk):
+        near_copy(0, chunk).wait_send()
+        near_copy(1, chunk).wait_send()
+        far_copy(chunk).wait_send()
+        for step in range(1, n_dp):
+            block_copy(chunk, lax.rem(dp + step, n_dp), dp).wait_send()
+
+
+def full_sum(value, rows, n_dp):
+    width = value.shape[-1]
+    own = width // n_dp
+    if own % 128 != 0:
+        return lax.psum_scatter(rep_sum(value, rows), "dp", scatter_dimension=1, tiled=True)
+    parts = value.reshape(4, -1, rows, width)
+    n_chunks = parts.shape[1]
+    block = (n_chunks, rows, width)
+    summed = pl.pallas_call(
+        functools.partial(full_sum_kernel, n_chunks, n_dp),
+        out_shape=jax.ShapeDtypeStruct((n_chunks, rows, own), jnp.bfloat16),
+        in_specs=[pl.BlockSpec(memory_space=pl.ANY)],
+        out_specs=pl.BlockSpec(memory_space=pltpu.VMEM),
+        scratch_shapes=[
+            pltpu.VMEM((2,) + block, jnp.bfloat16),
+            pltpu.VMEM((2,) + block, jnp.bfloat16),
+            pltpu.VMEM(block, jnp.bfloat16),
+            pltpu.VMEM(block, jnp.bfloat16),
+            pltpu.VMEM((n_chunks, n_dp, rows, own), jnp.bfloat16),
+            pltpu.SemaphoreType.DMA((2, n_chunks)),
+            pltpu.SemaphoreType.DMA((2, n_chunks)),
+            pltpu.SemaphoreType.DMA((2, n_chunks)),
+            pltpu.SemaphoreType.DMA((n_chunks,)),
+            pltpu.SemaphoreType.DMA((n_chunks,)),
+            pltpu.SemaphoreType.DMA((n_chunks, n_dp)),
+            pltpu.SemaphoreType.DMA((n_chunks, n_dp)),
+        ],
+        compiler_params=pltpu.CompilerParams(has_side_effects=True),
+        cost_estimate=pl.CostEstimate(
+            flops=value.size * 1000, bytes_accessed=value.size * 2, transcendentals=0
+        ),
+    )(parts)
+    return summed.reshape(n_chunks * rows, own)
+
+
 def column_block(matrix, source, width, rows=None):
     if len(matrix.shape) == 3:
         return matrix.at[source] if rows is None else matrix.at[source, rows]
@@ -234,12 +374,17 @@
 def spread_kernel(n_dp, matrix, out, held, owner_send, pair_send, far_send, recv, store_sem):
     dp = lax.axis_index("dp")
     rep = lax.axis_index("rep")
-    hidden, width = held.shape[1:]
+    half, width = held.shape[1:]
     owner = n_dp // 4
     pair = rep + 1 - 2 * lax.rem(rep, 2)
     other = lax.rem(rep + 2, 4)
     kinds = 3
-    matrices = [(expert, kind) for expert in range(2) for kind in range(kinds)]
+    matrices = {
+        2 * (kinds * expert + kind) + place: (expert, kind)
+        for place in range(2)
+        for expert in range(2)
+        for kind in range(kinds)
+    }
 
     def remote(source, index, send_sem, device):
         return pltpu.make_async_remote_copy(
@@ -254,24 +399,27 @@
     def store(index):
         return pltpu.make_async_copy(held.at[index], out.at[index], store_sem.at[index])
 
+    def rows_of(index):
+        return pl.ds(index % 2 * half, half)
+
     def root_of(expert, kind):
         return 2 * expert + kind % 2
 
-    for index, (expert, kind) in enumerate(matrices):
+    for index, (expert, kind) in matrices.items():
 
         @pl.when(jnp.logical_and(dp == owner + kind, rep == root_of(expert, kind)))
         def _(index=index, kind=kind):
-            for target in range(n_dp):
-                block = column_block(matrix, target, width)
+            for target in sorted(range(n_dp), key=lambda place: -abs(place - owner - kind)):
+                block = column_block(matrix, target, width, rows_of(index))
 
                 @pl.when(dp != target)
                 def _(target=target, block=block):
-                    remote(block, index, owner_send.at[target], (target, rep)).start()
+                    remote(block, index, owner_send.at[index % 2, target], (target, rep)).start()
 
                 @pl.when(dp == target)
                 def _(target=target, block=block):
                     pltpu.make_async_copy(
-                        block, held.at[index], owner_send.at[target]
+                        block, held.at[index], owner_send.at[index % 2, target]
                     ).start()
 
     def arrived(index, expert, kind):
@@ -280,16 +428,16 @@
         @pl.when(here)
         def _():
             pltpu.make_async_copy(
-                column_block(matrix, dp, width),
+                column_block(matrix, dp, width, rows_of(index)),
                 held.at[index],
-                owner_send.at[dp],
+                owner_send.at[index % 2, dp],
             ).wait()
 
         @pl.when(jnp.logical_not(here))
         def _():
             remote(held.at[index], index, pair_send.at[index], (dp, pair)).wait_recv()
 
-    for index, (expert, kind) in enumerate(matrices):
+    for index, (expert, kind) in matrices.items():
 
         @pl.when(rep == root_of(expert, kind))
         def _(index=index, expert=expert, kind=kind):
@@ -298,7 +446,7 @@
             remote(held.at[index], index, pair_send.at[index], (dp, pair)).start()
             store(index).start()
 
-    for index, (expert, kind) in enumerate(matrices):
+    for index, (expert, kind) in matrices.items():
 
         @pl.when(other == root_of(expert, kind))
         def _(index=index):
@@ -306,7 +454,7 @@
             remote(held.at[index], index, pair_send.at[index], (dp, pair)).start()
             store(index).start()
 
-    for index, (expert, kind) in enumerate(matrices):
+    for index, (expert, kind) in matrices.items():
         root = root_of(expert, kind)
 
         @pl.when(jnp.logical_and(rep != root, other != root))
@@ -314,7 +462,7 @@
             remote(held.at[index], index, pair_send.at[index], (dp, pair)).wait_recv()
             store(index).start()
 
-    for index, (expert, kind) in enumerate(matrices):
+    for index, (expert, kind) in matrices.items():
         root = root_of(expert, kind)
 
         @pl.when(jnp.logical_and(dp == owner + kind, rep == root))
@@ -324,9 +472,9 @@
                 @pl.when(dp != target)
                 def _(target=target):
                     remote(
-                        column_block(matrix, target, width),
+                        column_block(matrix, target, width, rows_of(index)),
                         index,
-                        owner_send.at[target],
+                        owner_send.at[index % 2, target],
                         (target, rep),
                     ).wait_send()
 
@@ -343,20 +491,21 @@
 
 def spread_matrix(matrix, n_dp):
     hidden, width = matrix.shape[0], matrix.shape[1] // n_dp
+    half = hidden // 2
     if width % 128 != 0:
         matrix = matrix.reshape(hidden, n_dp, width).transpose(1, 0, 2)
     return pl.pallas_call(
         functools.partial(spread_kernel, n_dp),
-        out_shape=jax.ShapeDtypeStruct((6, hidden, width), jnp.bfloat16),
+        out_shape=jax.ShapeDtypeStruct((12, half, width), jnp.bfloat16),
         in_specs=[pl.BlockSpec(memory_space=pltpu.VMEM)],
         out_specs=pl.BlockSpec(memory_space=pl.ANY),
         scratch_shapes=[
-            pltpu.VMEM((6, hidden, width), jnp.bfloat16),
-            pltpu.SemaphoreType.DMA((n_dp,)),
-            pltpu.SemaphoreType.DMA((6,)),
-            pltpu.SemaphoreType.DMA((6,)),
-            pltpu.SemaphoreType.DMA((6,)),
-            pltpu.SemaphoreType.DMA((6,)),
+            pltpu.VMEM((12, half, width), jnp.bfloat16),
+            pltpu.SemaphoreType.DMA((2, n_dp)),
+            pltpu.SemaphoreType.DMA((12,)),
+            pltpu.SemaphoreType.DMA((12,)),
+            pltpu.SemaphoreType.DMA((12,)),
+            pltpu.SemaphoreType.DMA((12,)),
         ],
         compiler_params=pltpu.CompilerParams(has_side_effects=True),
     )(matrix)
@@ -400,8 +549,8 @@
     weights_own = lax.all_gather(own_half, "dp", axis=2, tiled=True)
 
     row_place = jnp.arange(rows_here, dtype=jnp.int32) % block_rows
-    row_count = jnp.repeat(block_count, block_rows, total_repeat_length=rows_here)
-    row_expert = jnp.repeat(block_expert, block_rows, total_repeat_length=rows_here)
+    row_count = jnp.broadcast_to(block_count[:, None], (blocks, block_rows)).reshape(rows_here)
+    row_expert = jnp.broadcast_to(block_expert[:, None], (blocks, block_rows)).reshape(rows_here)
     live_rows = row_place < row_count
     masked = jnp.where(live_rows[:, None], cotangent, jnp.zeros_like(cotangent))
     gate = gate_preact.astype(jnp.float32)
@@ -435,8 +584,7 @@
     input_part = jnp.einsum(
         "erf,rd->efd", gate_up_each, token_inputs, preferred_element_type=jnp.float32
     ).astype(jnp.bfloat16)
-    input_sum = rep_sum(input_part, 128)
-    input_grad = lax.psum_scatter(input_sum, "dp", scatter_dimension=1, tiled=True)
+    input_grad = full_sum(input_part, 96, n_dp)
 
     whole = gather_matrix(input_grad, output_grad, n_dp)
     finished = whole_sweeps(whole, ITERS, jnp.sqrt(jnp.float32(D)))

time: 371 us -> 309 us (0.83)
  waiting for transfers between devices: 83.9 us -> 14.9 us
  Pallas kernels: 184 us -> 200 us
  other arithmetic: 17.2 us -> 12.5 us
    pallas_call x0 -> x1, Pallas kernels: none -> 94.3 us  [full_sum(): pl.pallas_call(functools.partial(full_sum_kernel, n_chunks, n_dp), out_sh...]
    pallas_call x2 -> x1, Pallas kernels: 123 us -> 47 us  [rep_sum(): pl.pallas_call(functools.partial(rep_sum_kernel, n_chunks), out_shape=jax...]
    reduce_scatter x1 -> x0, waiting for transfers between devices: 75.2 us -> none  [per_device(): lax.psum_scatter(input_sum, 'dp', scatter_dimension=1, tiled=True)]
    all_gather x1, waiting for transfers between devices: 2.73 us -> 8.9 us  [per_device(): weights_own = lax.all_gather(own_half, 'dp', axis=2, tiled=True)]
  transfers between devices with their start and end apart: 4 -> 3, of which waited for: 3 -> 2; matrix products, arithmetic and copies ran while one was open for 10% -> 10% of each run, Pallas kernels for 34% -> 46%
where the time goes in v2:
time: 309 us; the launch traced here: 306 us
  Pallas kernels  200 us (65%)
  matrix products  55.1 us (18%)
  waiting for transfers between devices  14.9 us (5%)
  between operations  14.2 us (5%)
  other arithmetic  12.5 us (4%)
  local copies, waits for them, and re-layouts  9.17 us (3%)
    pallas_call x1, Pallas kernels, full_sum(): pl.pallas_call(functools.partial(full_sum_kernel, n_chunks, n_dp), out_sh...  94.3 us
    pallas_call x1, Pallas kernels, rep_sum(): pl.pallas_call(functools.partial(rep_sum_kernel, n_chunks), out_shape=jax...  47 us
    pallas_call x1, Pallas kernels, spread_matrix(): pl.pallas_call(functools.partial(spread_kernel, n_dp), out_shape=jax.Shap...  38.7 us
    dot_general x2, matrix products, whole_sweeps(): jnp.dot(poly, current, preferred_element_type=jnp.float32)  21.4 us
    pallas_call x1, Pallas kernels, gather_matrix(): pl.pallas_call(functools.partial(gather_kernel, n_dp), out_shape=jax.Shap...  20.1 us
    dot_general x2, matrix products, whole_sweeps(): jnp.einsum('fd,gd->fg', current, current, preferred_element_type=jnp.floa...  13.8 us
    dot_general x1, matrix products, per_device(): jnp.einsum('erf,rd->efd', gate_up_each, token_inputs, preferred_element_t...  10.7 us
    all_gather x1, waiting for transfers between devices, per_device(): weights_own = lax.all_gather(own_half, 'dp', axis=2, tiled=True)  8.9 us
  transfers between devices with their start and end apart: 3, of which 2 were waited for; matrix products, arithmetic and copies ran while one was open for 10% of the time, Pallas kernels for 46%

profile of v2, /device:TPU:0, one launch (start us, length us, event | category | flops | bytes accessed | tf_op | source)
XLA Modules:
  0.0 306.0 jit_solution(1594622250887041320)
XLA Ops:
  6.5 0.0 copy-start
  6.5 0.0 all-gather.2.cloned.1.call-start
  6.5 1.9 constant_dynamic-slice_fusion
  8.5 0.0 copy-start.8
  8.5 0.0 copy-start.7
  8.5 0.0 all-gather.2.cloned.1.call-update
  8.5 0.0 reduce-scatter.2.cloned.1.call-start
  8.5 1.9 fusion.12
  10.4 1.2 copy.8
  11.6 0.0 copy-done.8
  11.6 0.0 copy-start.4
  11.6 0.1 fusion.33
  11.6 0.0 copy-done.7
  11.6 0.1 broadcast_bitcast_fusion
  11.7 1.9 broadcast_select_fusion.2
  13.6 0.0 copy-done.4
  13.6 0.0 copy-start.2
  13.6 5.3 %convolution_convert_fusion.1 = bf16[2,768,2048]{2,1,0:T(8,128)(2,1)} fusion(bf16[512,2048]{1,0:T(8,128)(2,1)S(1)} %broadcast_select_fusion.2, bf16[2,512]{1,0:T(2,128)(2,1)S(1)} %compare_convert_fusion, bf16[512,768]{0,1:T(8,128)(2,1)S(1)} %copy-done.4), kind=kOutput, calls=%fused_computation.11 | convolution fusion | flops 3225157632 | bytes 9177088 | tf_op jit(solution)/shard_map/erf,rd->efd/dot_general | solution.py:564
  18.9 0.0 copy-done.2
  18.9 47.0 %shard_map.73 = bf16[3,128,2048]{2,1,0:T(8,128)(2,1)} custom-call(bf16[4,3,128,2048]{3,2,1,0:T(8,128)(2,1)} %bitcast.25), custom_call_target="tpu_custom_call" | custom-call | flops 3145728000 | bytes 6291456 | tf_op jit(solution)/shard_map/pallas_call | solution.py:101
  65.9 8.9 %all-gather.2.cloned.1.call-done = bf16[2,384,2048]{2,1,0:T(8,128)(2,1)} async-done(((bf16[2,384,256]{2,1,0:T(8,128)(2,1)}), bf16[2,384,2048]{2,1,0:T(8,128)(2,1)}) %all-gather.2.cloned.1.call-update) | async-done | bytes 3145744 | tf_op jit(solution)/shard_map/all_gather | solution.py:549
  74.8 0.0 collective-permute-start
  74.8 0.0 reduce-scatter.2.cloned.1.call-update
  74.9 0.0 copy-start.3
  74.9 0.0 copy-start.5
  74.9 0.0 copy-start.6
  74.9 5.9 %collective-permute-done = bf16[2,384,2048]{2,1,0:T(8,128)(2,1)} collective-permute-done((bf16[2,384,2048]{2,1,0:T(8,128)(2,1)}, bf16[2,384,2048]{2,1,0:T(8,128)(2,1)}, u32[]{:S(2)}, u32[]{:S(2)}) %collective-permute-start) | collective-permute-done | bytes 3145760 | tf_op jit(solution)/shard_map/ppermute | solution.py:570
  80.8 3.3 %broadcast_select_fusion.1 = (bf16[2,384,2048]{2,1,0:T(8,128)(2,1)S(1)}, bf16[2,384,2048]{2,1,0:T(8,128)(2,1)S(1)}) fusion(bf16[2,384,2048]{2,1,0:T(8,128)(2,1)} %all-gather.2.cloned.1.call-done, bf16[2,384,2048]{2,1,0:T(8,128)(2,1)} %collective-permute-done, pred[]{:T(512)S(6)} %eq.29), kind=kLoop, calls=%fused_computation.15 | loop fusion | flops 3145728 | bytes 12582913 | tf_op jit(solution)/shard_map/jit(_where)/select_n | solution.py:574
  84.1 0.0 copy-done.3
  84.1 0.0 copy-done.5
  84.1 0.0 copy-done.6
  84.1 4.0 %fusion.15 = (bf16[512,768]{1,0:T(8,128)(2,1)S(1)}, bf16[512,768]{1,0:T(8,128)(2,1)S(1)}) fusion(bf16[512,768]{1,0:T(8,128)(2,1)S(1)} %copy-done.5, bf16[512,768]{1,0:T(8,128)(2,1)S(1)} %copy-done.6, bf16[2,384,2048]{2,1,0:T(8,128)(2,1)S(1)} %get-tuple-element.10, bf16[2,384,2048]{2,1,0:T(8,128)(2,1)S(1)} %get-tuple-element.9, ...), kind=kOutput, calls=%fused_computation.32 | convolution fusion | flops 3241803776 | bytes 11536384 | tf_op jit(solution)/shard_map/erd,efd->rf/dot_general | solution.py:577
  88.1 1.3 pad_maximum_fusion
  89.4 2.6 copy.9
  92.0 0.0 copy-done
  92.0 10.7 %convolution_convert_fusion = bf16[2,1536,2048]{2,1,0:T(8,128)(2,1)} fusion(bf16[512,2048]{1,0:T(8,128)(2,1)S(1)} %copy-done, bf16[2,512]{1,0:T(2,128)(2,1)S(1)} %compare_convert_fusion, bf16[512,1536]{0,1:T(8,128)(2,1)} %copy.9), kind=kOutput, calls=%fused_computation | convolution fusion | flops 6450315264 | bytes 16254976 | tf_op jit(solution)/shard_map/erf,rd->efd/dot_general | solution.py:584
  102.7 94.3 %shard_map.74 = bf16[8,96,256]{2,1,0:T(8,128)(2,1)} custom-call(bf16[4,8,96,2048]{3,2,1,0:T(8,128)(2,1)} %bitcast.24), custom_call_target="tpu_custom_call" | custom-call | flops 6291456000 | bytes 12582912 | tf_op jit(solution)/shard_map/pallas_call | solution.py:239
  197.0 0.0 reduce-scatter.2.cloned.1.call-done.second
  197.0 20.1 %shard_map.75 = bf16[768,2048]{1,0:T(8,128)(2,1)} custom-call(bf16[768,256]{1,0:T(8,128)(2,1)} %bitcast.23, bf16[384,256]{1,0:T(8,128)(2,1)} %reduce-scatter.2.cloned.1.call-done.second), custom_call_target="tpu_custom_call" | custom-call | tf_op jit(solution)/shard_map/pallas_call | solution.py:358
  217.1 4.1 %fusion = f32[]{:T(128)} fusion(bf16[768,2048]{1,0:T(8,128)(2,1)} %shard_map.75), kind=kLoop, calls=%fused_computation.3 | loop fusion | flops 4718591 | bytes 3145732 | tf_op jit(solution)/shard_map/reduce_sum | solution.py:516
  221.9 6.9 %fusion.42 = f32[768,768]{1,0:T(8,128)} fusion(bf16[768,2048]{1,0:T(8,128)(2,1)} %shard_map.75, f32[]{:T(128)S(6)} %add.40), kind=kOutput, calls=%fused_computation.61 | convolution fusion | flops 2420637696 | bytes 5505028 | tf_op jit(solution)/shard_map/fd,gd->fg/dot_general | solution.py:520
  228.8 11.2 %add_convert_fusion = bf16[768,2048]{1,0:T(8,128)(2,1)} fusion(f32[768,768]{1,0:T(8,128)} %fusion.42, f32[]{:T(128)S(6)} %add.40, bf16[768,2048]{1,0:T(8,128)(2,1)} %shard_map.75), kind=kOutput, calls=%fused_computation.10 | convolution fusion | flops 3340566528 | bytes 8650756 | tf_op jit(solution)/shard_map/dot_general | solution.py:524
  240.0 6.9 %fusion.45 = f32[768,768]{1,0:T(8,128)} fusion(bf16[768,2048]{1,0:T(8,128)(2,1)} %add_convert_fusion), kind=kOutput, calls=%fused_computation.62 | convolution fusion | flops 2415919104 | bytes 5505024 | tf_op jit(solution)/shard_map/fd,gd->fg/dot_general | solution.py:520
  247.0 10.2 %multiply_convert_fusion.matrix = bf16[768,2048]{1,0:T(8,128)(2,1)} fusion(bf16[768,2048]{1,0:T(8,128)(2,1)} %add_convert_fusion, f32[768,768]{1,0:T(8,128)} %fusion.45), kind=kOutput, calls=%fused_computation.9 | convolution fusion | flops 3332702208 | bytes 8650752 | tf_op jit(solution)/shard_map/dot_general | solution.py:524
  257.1 38.7 %shard_map.76 = bf16[12,384,256]{2,1,0:T(8,128)(2,1)} custom-call(bf16[768,2048]{1,0:T(8,128)(2,1)} %multiply_convert_fusion.matrix), custom_call_target="tpu_custom_call" | custom-call | tf_op jit(solution)/shard_map/pallas_call | solution.py:497
  295.8 0.0 copy-start.1
  295.8 3.4 %copy.11 = bf16[2,3,768,256]{3,2,1,0:T(8,128)(2,1)} copy(bf16[2,3,768,256]{3,2,1,0:T(8,128)(2,1)} %bitcast.21) | data formatting | bytes 4718592
  299.2 0.0 copy-done.1
  (1 shorter events, 0.0 us)
Async XLA Ops:
  6.5 85.5 %copy-start = (bf16[512,2048]{1,0:T(8,128)(2,1)S(1)}, bf16[512,2048]{1,0:T(8,128)(2,1)}, u32[]{:S(2)}) copy-start(bf16[512,2048]{1,0:T(8,128)(2,1)} %param.7) | copy-start | bytes 6291460
  6.5 68.3 %all-gather.2.cloned.1.call-start = ((), (), s32[]{:S(2)}) async-start(), calls=%async_computation.1 | async-start | bytes 3538944 | tf_op jit(solution)/shard_map/all_gather | solution.py:549
  8.5 3.1 %copy-start.8 = (s32[4]{0:T(128)S(1)}, s32[4]{0:T(128)}, u32[]{:S(2)}) copy-start(s32[4]{0:T(128)} %param.13) | copy-start | bytes 52
  8.5 3.2 %copy-start.7 = (s32[4]{0:T(128)S(1)}, s32[4]{0:T(128)}, u32[]{:S(2)}) copy-start(s32[4]{0:T(128)} %param.12) | copy-start | bytes 52
  8.5 188.5 %reduce-scatter.2.cloned.1.call-start = ((), (), s32[]{:S(2)}) async-start(), calls=%async_computation.2 | async-start | bytes 1769472 | tf_op jit(solution)/shard_map/reduce_scatter | solution.py:571
  11.6 2.0 copy-start.4
  13.6 5.3 %copy-start.2 = (bf16[512,2048]{1,0:T(8,128)(2,1)}, bf16[512,2048]{1,0:T(8,128)(2,1)S(1)}, u32[]{:S(2)}) copy-start(bf16[512,2048]{1,0:T(8,128)(2,1)S(1)} %broadcast_select_fusion.2) | copy-start | bytes 6291460
  74.8 6.0 %collective-permute-start = (bf16[2,384,2048]{2,1,0:T(8,128)(2,1)}, bf16[2,384,2048]{2,1,0:T(8,128)(2,1)}, u32[]{:S(2)}, u32[]{:S(2)}) collective-permute-start(bf16[2,384,2048]{2,1,0:T(8,128)(2,1)} %all-gather.2.cloned.1.call-done), channel_id=1, source_target_pairs={{0,1},{1,0},{2,3},{3,2},{4,5},{5,4},{6,7},{7,6},{8,9},{9,8},{10,11... | collective-permute-start | bytes 9437192 | tf_op jit(solution)/shard_map/ppermute | solution.py:570
  74.9 9.2 %copy-start.3 = (bf16[512,2048]{1,0:T(8,128)(2,1)S(1)}, bf16[512,2048]{1,0:T(8,128)(2,1)}, u32[]{:S(2)}) copy-start(bf16[512,2048]{1,0:T(8,128)(2,1)} %copy-done.2) | copy-start | bytes 6291460
  74.9 9.2 %copy-start.5 = (bf16[512,768]{1,0:T(8,128)(2,1)S(1)}, bf16[512,768]{1,0:T(8,128)(2,1)}, u32[]{:S(2)}) copy-start(bf16[512,768]{1,0:T(8,128)(2,1)} %param.10) | copy-start | bytes 2359300
  74.9 9.2 %copy-start.6 = (bf16[512,768]{1,0:T(8,128)(2,1)S(1)}, bf16[512,768]{1,0:T(8,128)(2,1)}, u32[]{:S(2)}) copy-start(bf16[512,768]{1,0:T(8,128)(2,1)} %param.9) | copy-start | bytes 2359300
  295.8 3.4 %copy-start.1 = (bf16[512,2048]{1,0:T(8,128)(2,1)S(1)}, bf16[512,2048]{1,0:T(8,128)(2,1)}, u32[]{:S(2)}) copy-start(bf16[512,2048]{1,0:T(8,128)(2,1)} %param.7) | copy-start | bytes 6291460
Sparse Core Ops, SparseCore 0:
  9.4 65.4 all-gather.1
  78.3 71.7 reduce-scatter.1
